TPU v7x, 32 devices: a whole 2x2x4 slice. The times are simulated.
32 devices in a mesh: freq: 8 (over z, y), cell: 4 (over x, core).
Axes of the slice: x: 2, y: 2, z: 4, core: 2. Of those that a mesh axis runs over, the one named last changes fastest.
Arguments:
- columns: float32 [2, 16, 64, 600], P(None, 'freq'), may hold values from -6 to 6
- freq_blocks: float32 [2, 16, 600, 1024], P(None, 'freq', None, 'cell'), may hold values from -0.1875 to 0.1875
- causal_cutoffs: int32 [64], replicated, may hold values from 3 to 15
- band_index: int32 [1024], P('cell'), may hold values from 0 to 7
- band_rates: float32 [8], replicated, may hold values from 0.05 to 0.45
Outputs:
- hessian_columns: float32 [2, 16, 64, 600], P(None, 'freq', 'cell')
All inputs are finite; a program needn't handle non-finite values.
Results may differ from a plain program's by a relative error of at most 0.00007.
Values sent between devices are 32-bit elements; how exact they have to be, the bound alone decides.
No kernel may reach another device: no remote copies, remote signals or barrier semaphores. Data moves between devices by JAX's collectives and lax.ppermute only.
A program may use at most 64 MiB of HBM per device.

v0:
```python
import math

import jax
import jax.numpy as jnp
from jax import lax
from jax.sharding import PartitionSpec as P

MODE_SHARE_WIDTH = 8
C_DEV = 256
SWEEPS = 4
BANDS = 8


precise = lax.Precision.HIGHEST


def extended(shard, sides, width):
    for axis, dim in sides:
        devices, length = (lax.axis_size(axis), shard.shape[dim])
        up = [(i, (i + 1) % devices) for i in range(devices - 1)]
        down = [(j, i) for i, j in up]
        last = lax.slice_in_dim(shard, length - width, length, axis=dim)
        leading = lax.slice_in_dim(shard, 0, width, axis=dim)
        before = lax.ppermute(last, axis, up)
        after = lax.ppermute(leading, axis, down)
        shard = jnp.concatenate([before, shard, after], axis=dim)
    return shard


def inverse_table(epoch_number, harmonic_number):
    cycle_length = 2 * epoch_number
    sample_moments = lax.broadcasted_iota(jnp.int32, (epoch_number, harmonic_number), 0)
    harmonic_rate = lax.broadcasted_iota(jnp.int32, (epoch_number, harmonic_number), 1)
    harmonic_offsets = (sample_moments * harmonic_rate % cycle_length).astype(jnp.float32) * (
        2.0 * math.pi / cycle_length
    )
    weight = (
        jnp.where((harmonic_rate == 0) | (harmonic_rate == harmonic_number - 1), 1.0, 2.0).astype(
            jnp.float32
        )
        / cycle_length
    )
    return jnp.concatenate(
        [weight * jnp.cos(harmonic_offsets), -weight * jnp.sin(harmonic_offsets)], axis=1
    )


def forward_table(epoch_number, harmonic_number):
    cycle_length = 2 * epoch_number
    harmonic_rate = lax.broadcasted_iota(jnp.int32, (harmonic_number, epoch_number), 0)
    sample_moments = lax.broadcasted_iota(jnp.int32, (harmonic_number, epoch_number), 1)
    harmonic_offsets = (sample_moments * harmonic_rate % cycle_length).astype(jnp.float32) * (
        2.0 * math.pi / cycle_length
    )
    return jnp.concatenate([jnp.cos(harmonic_offsets), -jnp.sin(harmonic_offsets)], axis=0)


def adjoint_product(columns, blocks):
    real_part = jnp.einsum("kjs,ksm->kjm", columns[0], blocks[0], precision=precise) + jnp.einsum(
        "kjs,ksm->kjm", columns[1], blocks[1], precision=precise
    )
    imag_part = jnp.einsum("kjs,ksm->kjm", columns[1], blocks[0], precision=precise) - jnp.einsum(
        "kjs,ksm->kjm", columns[0], blocks[1], precision=precise
    )
    return jnp.stack([real_part, imag_part])


def forward_product(spectrum, blocks):
    real_part = jnp.einsum("kjm,ksm->kjs", spectrum[0], blocks[0], precision=precise) - jnp.einsum(
        "kjm,ksm->kjs", spectrum[1], blocks[1], precision=precise
    )
    imag_part = jnp.einsum("kjm,ksm->kjs", spectrum[1], blocks[0], precision=precise) + jnp.einsum(
        "kjm,ksm->kjs", spectrum[0], blocks[1], precision=precise
    )
    return jnp.stack([real_part, imag_part])


def on_device(columns, freq_blocks, causal_cutoffs, band_index, band_rates):
    col_total = columns.shape[2]
    local_spectrum = adjoint_product(columns, freq_blocks)
    gathered = lax.all_to_all(local_spectrum, "freq", split_axis=2, concat_axis=1, tiled=True)
    freq_total = gathered.shape[1]
    horizon_span = freq_total - 1
    sampled_trace = jnp.dot(
        inverse_table(horizon_span, freq_total),
        gathered.reshape(2 * freq_total, MODE_SHARE_WIDTH * C_DEV),
        precision=precise,
        preferred_element_type=jnp.float32,
    )
    sampled_trace = sampled_trace.reshape(horizon_span, MODE_SHARE_WIDTH, C_DEV)
    device_ranges = lax.dynamic_slice_in_dim(
        causal_cutoffs, lax.axis_index("freq") * MODE_SHARE_WIDTH, MODE_SHARE_WIDTH
    )
    sample_moments = lax.broadcasted_iota(jnp.int32, (horizon_span, MODE_SHARE_WIDTH), 0)
    sampled_trace = jnp.where(
        (sample_moments < device_ranges[None, :])[:, :, None], sampled_trace, 0.0
    )
    flat = sampled_trace.reshape(horizon_span * MODE_SHARE_WIDTH, C_DEV)
    levels = lax.broadcasted_iota(jnp.int32, (BANDS, C_DEV), 0)
    cell_rates = jnp.sum(jnp.where(levels == band_index[None, :], band_rates[:, None], 0.0), axis=0)
    stacked = jnp.concatenate([flat, cell_rates[None, :]], axis=0)
    padded = extended(stacked, (("cell", 1),), SWEEPS)
    field = padded[:-1]
    margin_rates = padded[-1]
    for repeat in range(SWEEPS):
        inner_rates = margin_rates[1:-1]
        field = field[:, 1:-1] + inner_rates * (field[:, :-2] - 2.0 * field[:, 1:-1] + field[:, 2:])
        margin_rates = inner_rates
    flat = field
    spectrum = jnp.dot(
        forward_table(horizon_span, freq_total),
        flat.reshape(horizon_span, MODE_SHARE_WIDTH * C_DEV),
        precision=precise,
        preferred_element_type=jnp.float32,
    )
    spectrum = spectrum.reshape(2, freq_total, MODE_SHARE_WIDTH, C_DEV)
    returned = lax.all_to_all(spectrum, "freq", split_axis=1, concat_axis=2, tiled=True)
    partial_terms = forward_product(returned, freq_blocks)
    totals = lax.psum(partial_terms, "cell")
    share = col_total // lax.axis_size("cell")
    return lax.dynamic_slice_in_dim(totals, lax.axis_index("cell") * share, share, 2)


def solution(mesh):
    placed = (P(None, "freq", None, None), P(None, "freq", None, "cell"), P(), P("cell"), P())
    return jax.shard_map(
        on_device,
        mesh=mesh,
        in_specs=placed,
        out_specs=P(None, "freq", "cell", None),
        check_vma=False,
    )
```

profile of v0, /device:TPU:0, one launch (start us, length us, event | category | flops | bytes accessed | tf_op | source)
XLA Modules:
  0.0 98.5 jit_solution(15903029011630750266)
XLA Ops:
  6.5 2.4 %fusion.4 = f32[2,64,256]{2,1,0:T(8,128)S(1)} fusion(f32[2,2,600,256]{3,2,1,0:T(8,128)} %param.6, f32[2,2,64,600]{3,2,1,0:T(8,128)} %param.5), kind=kOutput, calls=%fused_computation.4 | convolution fusion | flops 235929600 | bytes 1687552 | tf_op jit(solution)/shard_map/kjs,ksm->kjm/dot_general | solution.py:62
  9.0 2.3 %fusion.6 = f32[2,64,256]{2,1,0:T(8,128)S(1)} fusion(f32[2,2,600,256]{3,2,1,0:T(8,128)} %param.6, f32[2,2,64,600]{3,2,1,0:T(8,128)} %param.5), kind=kOutput, calls=%fused_computation.6 | convolution fusion | flops 235929600 | bytes 1687552 | tf_op jit(solution)/shard_map/kjs,ksm->kjm/dot_general | solution.py:59
  11.4 0.9 fusion.37
  12.3 0.9 fusion.31
  13.2 0.9 copy.21
  14.1 7.3 %all-to-all-start = ((f32[2,2,64,256]{3,1,0,2:T(2,128)}), f32[2,2,64,256]{3,1,0,2:T(2,128)S(1)}, u32[]{:S(2)}, u32[]{:S(2)}) async-start(f32[2,2,64,256]{3,1,0,2:T(2,128)} %copy.21), calls=%async_computation | async-start | bytes 524288 | tf_op jit(solution)/shard_map/all_to_all | solution.py:81
  21.9 8.5 %all-to-all-done = f32[2,2,64,256]{3,1,0,2:T(2,128)S(1)} async-done(((f32[2,2,64,256]{3,1,0,2:T(2,128)}), f32[2,2,64,256]{3,1,0,2:T(2,128)S(1)}, u32[]{:S(2)}, u32[]{:S(2)}) %all-to-all-start) | async-done | bytes 262176 | tf_op jit(solution)/shard_map/all_to_all | solution.py:81
  30.4 0.3 convolution_select_fusion
  30.9 1.3 %collective-permute-start = (f32[121,4]{1,0:T(8,128)S(1)}, f32[121,4]{1,0:T(8,128)S(1)}, u32[]{:S(2)}, u32[]{:S(2)}) collective-permute-start(f32[121,4]{1,0:T(8,128)S(1)} %get-tuple-element.5), channel_id=1, source_target_pairs={{0,1},{1,2},{2,3},{4,5},{5,6},{6,7},{8,9},{9,10},{10,11},{12,13},{... | collective-permute-start | bytes 5816 | tf_op jit(solution)/shard_map/ppermute | solution.py:24
  32.2 1.3 %collective-permute-start.1 = (f32[121,4]{1,0:T(8,128)S(1)}, f32[121,4]{1,0:T(8,128)S(1)}, u32[]{:S(2)}, u32[]{:S(2)}) collective-permute-start(f32[121,4]{1,0:T(8,128)S(1)} %get-tuple-element.6), channel_id=1, source_target_pairs={{1,0},{2,1},{3,2},{5,4},{6,5},{7,6},{9,8},{10,9},{11,10},{13,12},{... | collective-permute-start | bytes 5816 | tf_op jit(solution)/shard_map/ppermute | solution.py:25
  33.5 3.5 %collective-permute-done.1 = f32[121,4]{1,0:T(8,128)S(1)} collective-permute-done((f32[121,4]{1,0:T(8,128)S(1)}, f32[121,4]{1,0:T(8,128)S(1)}, u32[]{:S(2)}, u32[]{:S(2)}) %collective-permute-start.1) | collective-permute-done | bytes 1968 | tf_op jit(solution)/shard_map/ppermute | solution.py:25
  37.3 0.2 fusion.63
  37.6 0.2 fusion.61
  37.8 0.2 fusion.59
  38.2 0.4 fusion.64
  38.6 0.2 copy.26
  38.8 11.7 %all_to_all.30 = f32[2,16,8,256]{3,2,0,1:T(8,128)S(1)} all-to-all(f32[2,16,8,256]{3,2,0,1:T(8,128)S(1)} %copy.26), channel_id=1, replica_groups=mesh['freq'=8,'cell'=4] {'freq'}, dimensions={1} | all-to-all | bytes 524288 | tf_op jit(solution)/shard_map/all_to_all | solution.py:117
  50.5 1.2 %fusion = f32[2,64,600]{2,1,0:T(8,128)S(1)} fusion(f32[2,2,600,256]{3,2,1,0:T(8,128)S(1)} %copy-done, f32[2,2,8,8,256]{4,3,2,1,0:T(8,128)S(1)} %bitcast.106), kind=kOutput, calls=%fused_computation | convolution fusion | flops 235929600 | bytes 1667072 | tf_op jit(solution)/shard_map/kjm,ksm->kjs/dot_general | solution.py:72
  51.7 1.2 %fusion.2 = f32[2,64,600]{2,1,0:T(8,128)S(1)} fusion(f32[2,2,600,256]{3,2,1,0:T(8,128)S(1)} %copy-done, f32[2,2,8,8,256]{4,3,2,1,0:T(8,128)S(1)} %bitcast.107), kind=kOutput, calls=%fused_computation.2 | convolution fusion | flops 235929600 | bytes 1667072 | tf_op jit(solution)/shard_map/kjm,ksm->kjs/dot_general | solution.py:69
  52.9 1.2 %fusion.22 = f32[1,2,64,600]{3,2,1,0:T(8,128)S(1)} fusion(f32[2,64,600]{2,1,0:T(8,128)S(1)} %fusion, f32[2,2,600,256]{3,2,1,0:T(8,128)S(1)} %copy-done, f32[2,2,8,8,256]{4,3,2,1,0:T(8,128)S(1)} %bitcast.108), kind=kOutput, calls=%fused_computation.18 | convolution fusion | flops 236006400 | bytes 1994752 | tf_op jit(solution)/shard_map/kjm,ksm->kjs/dot_general | solution.py:72
  54.2 1.2 %fusion.25 = f32[1,2,64,600]{3,2,1,0:T(8,128)S(1)} fusion(f32[2,64,600]{2,1,0:T(8,128)S(1)} %fusion.2, f32[2,2,600,256]{3,2,1,0:T(8,128)S(1)} %copy-done, f32[2,2,8,8,256]{4,3,2,1,0:T(8,128)S(1)} %bitcast.109), kind=kOutput, calls=%fused_computation.19 | convolution fusion | flops 236006400 | bytes 1994752 | tf_op jit(solution)/shard_map/kjm,ksm->kjs/dot_general | solution.py:69
  55.4 0.9 pad_maximum_fusion
  56.3 33.7 %all-reduce.2.cloned.1.call-done = f32[2,2,64,600]{3,2,1,0:T(8,128)} async-done(((f32[2,2,64,600]{3,2,1,0:T(8,128)}), f32[2,2,64,600]{3,2,1,0:T(8,128)}) %all-reduce.2.cloned.1.call-update) | async-done | bytes 614416 | tf_op jit(solution)/shard_map/psum | solution.py:119
  90.1 1.6 %constant_dynamic-slice_fusion = f32[2,2,16,600]{3,2,1,0:T(8,128)} fusion(f32[2,2,64,600]{3,2,1,0:T(8,128)} %all-reduce.2.cloned.1.call-done, s32[]{:T(128)S(6)} %select_n.44), kind=kLoop, calls=%fused_computation.104 | loop fusion | bytes 307204 | tf_op jit(solution)/shard_map/dynamic_slice | solution.py:121
  (34 shorter events, 1.3 us)
Async XLA Ops:
  6.5 4.8 %copy-start = (f32[2,2,600,256]{3,2,1,0:T(8,128)S(1)}, f32[2,2,600,256]{3,2,1,0:T(8,128)}, u32[]{:S(2)}) copy-start(f32[2,2,600,256]{3,2,1,0:T(8,128)} %param.6) | copy-start | bytes 7372804
  6.5 4.8 %copy-start.1 = (f32[2,2,64,600]{3,2,1,0:T(8,128)S(1)}, f32[2,2,64,600]{3,2,1,0:T(8,128)}, u32[]{:S(2)}) copy-start(f32[2,2,64,600]{3,2,1,0:T(8,128)} %param.5) | copy-start | bytes 1843204
  11.3 10.2 %copy-start.2 = (s32[256]{0:T(256)S(1)}, s32[256]{0:T(256)}, u32[]{:S(2)}) copy-start(s32[256]{0:T(256)} %param.8) | copy-start | bytes 3076
  11.3 10.2 %copy-start.3 = (f32[8]{0:T(128)S(1)}, f32[8]{0:T(128)}, u32[]{:S(2)}) copy-start(f32[8]{0:T(128)} %param.9) | copy-start | bytes 100
  11.3 10.3 %copy-start.4 = (s32[64]{0:T(128)S(1)}, s32[64]{0:T(128)}, u32[]{:S(2)}) copy-start(s32[64]{0:T(128)} %param.7) | copy-start | bytes 772
  14.1 16.2 %all-to-all-start = ((f32[2,2,64,256]{3,1,0,2:T(2,128)}), f32[2,2,64,256]{3,1,0,2:T(2,128)S(1)}, u32[]{:S(2)}, u32[]{:S(2)}) async-start(f32[2,2,64,256]{3,1,0,2:T(2,128)} %copy.21), calls=%async_computation | async-start | bytes 524288 | tf_op jit(solution)/shard_map/all_to_all | solution.py:81
  21.4 68.7 %all-reduce.2.cloned.1.call-start = ((), (), s32[]{:S(2)}) async-start(), calls=%async_computation.2 | async-start | bytes 1310720 | tf_op jit(solution)/shard_map/psum | solution.py:119
  30.9 2.6 %collective-permute-start = (f32[121,4]{1,0:T(8,128)S(1)}, f32[121,4]{1,0:T(8,128)S(1)}, u32[]{:S(2)}, u32[]{:S(2)}) collective-permute-start(f32[121,4]{1,0:T(8,128)S(1)} %get-tuple-element.5), channel_id=1, source_target_pairs={{0,1},{1,2},{2,3},{4,5},{5,6},{6,7},{8,9},{9,10},{10,11},{12,13},{... | collective-permute-start | bytes 5816 | tf_op jit(solution)/shard_map/ppermute | solution.py:24
  32.2 4.9 %collective-permute-start.1 = (f32[121,4]{1,0:T(8,128)S(1)}, f32[121,4]{1,0:T(8,128)S(1)}, u32[]{:S(2)}, u32[]{:S(2)}) collective-permute-start(f32[121,4]{1,0:T(8,128)S(1)} %get-tuple-element.6), channel_id=1, source_target_pairs={{1,0},{2,1},{3,2},{5,4},{6,5},{7,6},{9,8},{10,9},{11,10},{13,12},{... | collective-permute-start | bytes 5816 | tf_op jit(solution)/shard_map/ppermute | solution.py:25
Sparse Core Ops, SparseCore 0:
  56.5 33.5 all-reduce.1
where the time goes:
time: 98.8 us; the launch traced here: 98.5 us
  waiting for transfers between devices  45.8 us (46%)
  between operations  13.7 us (14%)
  matrix products  12.1 us (12%)
  blocking collectives  11.7 us (12%)
  starting transfers between devices  9.93 us (10%)
  local copies, waits for them, and re-layouts  2.98 us (3%)
  other arithmetic  2.33 us (2%)
    psum x1, waiting for transfers between devices, on_device(): totals = lax.psum(partial_terms, 'cell')  33.7 us
    all_to_all x1, blocking collectives, on_device(): lax.all_to_all(spectrum, 'freq', split_axis=1, concat_axis=2, tiled=True)  11.7 us
    all_to_all x1, waiting for transfers between devices, on_device(): lax.all_to_all(local_spectrum, 'freq', split_axis=2, concat_axis=1, tiled...  8.46 us
    all_to_all x1, starting transfers between devices, on_device(): lax.all_to_all(local_spectrum, 'freq', split_axis=2, concat_axis=1, tiled...  7.31 us
    ppermute x1, waiting for transfers between devices, extended(): after = lax.ppermute(leading, axis, down)  3.54 us
    dot_general x1, matrix products, adjoint_product(): jnp.einsum('kjs,ksm->kjm', columns[0], blocks[1], precision=precise)  2.44 us
    dot_general x1, matrix products, adjoint_product(): jnp.einsum('kjs,ksm->kjm', columns[1], blocks[1], precision=precise)  2.3 us
  transfers between devices with their start and end apart: 4, of which 3 were waited for; matrix products, arithmetic and copies ran while one was open for 0% of the time, Pallas kernels for 0%

commit v1 on v0

--- a/solution.py
+++ b/solution.py
@@ -116,9 +116,10 @@
     spectrum = spectrum.reshape(2, freq_total, MODE_SHARE_WIDTH, C_DEV)
     returned = lax.all_to_all(spectrum, "freq", split_axis=1, concat_axis=2, tiled=True)
     partial_terms = forward_product(returned, freq_blocks)
-    totals = lax.psum(partial_terms, "cell")
     share = col_total // lax.axis_size("cell")
-    return lax.dynamic_slice_in_dim(totals, lax.axis_index("cell") * share, share, 2)
+    blocks = partial_terms.reshape(partial_terms.shape[:2] + (lax.axis_size("cell"), share, partial_terms.shape[3]))
+    mine = lax.all_to_all(blocks, "cell", split_axis=2, concat_axis=2, tiled=True)
+    return jnp.sum(mine, axis=2)
 
 
 def solution(mesh):

time: 98.8 us -> 64 us (0.65)
  waiting for transfers between devices: 45.8 us -> 12.1 us
  blocking collectives: 11.7 us -> 25.7 us
  between operations: 13.7 us -> 0.29 us
  local copies, waits for them, and re-layouts: 2.98 us -> 1.43 us
    psum x1 -> x0, waiting for transfers between devices: 33.7 us -> none  [on_device(): totals = lax.psum(partial_terms, 'cell')]
    all_to_all x0 -> x1, blocking collectives: none -> 14 us  [on_device(): lax.all_to_all(blocks, 'cell', split_axis=2, concat_axis=2, tiled=True)]
    dynamic_slice x1 -> x0, local copies, waits for them, and re-layouts: 1.59 us -> none  [on_device(): lax.dynamic_slice_in_dim(totals, lax.axis_index('cell') * share, share, 2)]
  transfers between devices with their start and end apart: 4 -> 3, of which waited for: 3 -> 2; matrix products, arithmetic and copies ran while one was open for 0% -> 1% of each run, Pallas kernels for 0% -> 0%
where the time goes in v1:
time: 64 us; the launch traced here: 63.7 us
  blocking collectives  25.7 us (40%)
  matrix products  12.1 us (19%)
  waiting for transfers between devices  12.1 us (19%)
  starting transfers between devices  9.89 us (15%)
  other arithmetic  2.18 us (3%)
  local copies, waits for them, and re-layouts  1.43 us (2%)
    all_to_all x1, blocking collectives, on_device(): lax.all_to_all(blocks, 'cell', split_axis=2, concat_axis=2, tiled=True)  14 us
    all_to_all x1, blocking collectives, on_device(): lax.all_to_all(spectrum, 'freq', split_axis=1, concat_axis=2, tiled=True)  11.7 us
    all_to_all x1, waiting for transfers between devices, on_device(): lax.all_to_all(local_spectrum, 'freq', split_axis=2, concat_axis=1, tiled...  8.51 us
    all_to_all x1, starting transfers between devices, on_device(): lax.all_to_all(local_spectrum, 'freq', split_axis=2, concat_axis=1, tiled...  7.31 us
    ppermute x1, waiting for transfers between devices, extended(): after = lax.ppermute(leading, axis, down)  3.56 us
    dot_general x1, matrix products, adjoint_product(): jnp.einsum('kjs,ksm->kjm', columns[0], blocks[1], precision=precise)  2.44 us
    dot_general x1, matrix products, adjoint_product(): jnp.einsum('kjs,ksm->kjm', columns[1], blocks[1], precision=precise)  2.3 us
    ppermute x1, starting transfers between devices, extended(): after = lax.ppermute(leading, axis, down)  1.29 us
  transfers between devices with their start and end apart: 3, of which 2 were waited for; matrix products, arithmetic and copies ran while one was open for 1% of the time, Pallas kernels for 0%

profile of v1, /device:TPU:0, one launch (start us, length us, event | category | flops | bytes accessed | tf_op | source)
XLA Modules:
  0.0 63.7 jit_solution(2805120574086009828)
XLA Ops:
  0.0 2.4 %fusion.4 = f32[2,64,256]{2,1,0:T(8,128)S(1)} fusion(f32[2,2,600,256]{3,2,1,0:T(8,128)} %param.6, f32[2,2,64,600]{3,2,1,0:T(8,128)} %param.5), kind=kOutput, calls=%fused_computation.4 | convolution fusion | flops 235929600 | bytes 1687552 | tf_op jit(solution)/shard_map/kjs,ksm->kjm/dot_general | solution.py:62
  2.4 2.3 %fusion.6 = f32[2,64,256]{2,1,0:T(8,128)S(1)} fusion(f32[2,2,600,256]{3,2,1,0:T(8,128)} %param.6, f32[2,2,64,600]{3,2,1,0:T(8,128)} %param.5), kind=kOutput, calls=%fused_computation.6 | convolution fusion | flops 235929600 | bytes 1687552 | tf_op jit(solution)/shard_map/kjs,ksm->kjm/dot_general | solution.py:59
  4.8 0.9 %fusion.31 = f32[1,2,64,256]{3,2,1,0:T(8,128)S(1)} fusion(f32[2,64,256]{2,1,0:T(8,128)S(1)} %fusion.4, f32[2,2,600,256]{3,2,1,0:T(8,128)S(1)} %copy-done, f32[2,2,64,600]{3,2,1,0:T(8,128)S(1)} %copy-done.1), kind=kOutput, calls=%fused_computation.21 | convolution fusion | flops 235962368 | bytes 1818624 | tf_op jit(solution)/shard_map/kjs,ksm->kjm/dot_general | solution.py:62
  5.7 0.9 %fusion.25 = f32[1,2,64,256]{3,2,1,0:T(8,128)S(1)} fusion(f32[2,64,256]{2,1,0:T(8,128)S(1)} %fusion.6, f32[2,2,600,256]{3,2,1,0:T(8,128)S(1)} %copy-done, f32[2,2,64,600]{3,2,1,0:T(8,128)S(1)} %copy-done.1), kind=kOutput, calls=%fused_computation.19 | convolution fusion | flops 235962368 | bytes 1818624 | tf_op jit(solution)/shard_map/kjs,ksm->kjm/dot_general | solution.py:59
  6.7 0.9 %copy.23 = f32[2,2,64,256]{3,1,0,2:T(2,128)} copy(f32[2,2,64,256]{3,2,1,0:T(8,128)S(1)} %pad_maximum_fusion.1) | data formatting | bytes 524288 | tf_op jit(solution)/shard_map/stack | solution.py:65
  7.6 7.3 %all-to-all-start = ((f32[2,2,64,256]{3,1,0,2:T(2,128)}), f32[2,2,64,256]{3,1,0,2:T(2,128)S(1)}, u32[]{:S(2)}, u32[]{:S(2)}) async-start(f32[2,2,64,256]{3,1,0,2:T(2,128)} %copy.23), calls=%async_computation | async-start | bytes 524288 | tf_op jit(solution)/shard_map/all_to_all | solution.py:81
  15.3 8.5 %all-to-all-done = f32[2,2,64,256]{3,1,0,2:T(2,128)S(1)} async-done(((f32[2,2,64,256]{3,1,0,2:T(2,128)}), f32[2,2,64,256]{3,1,0,2:T(2,128)S(1)}, u32[]{:S(2)}, u32[]{:S(2)}) %all-to-all-start) | async-done | bytes 262176 | tf_op jit(solution)/shard_map/all_to_all | solution.py:81
  23.9 0.3 convolution_select_fusion
  24.4 1.3 %collective-permute-start = (f32[121,4]{1,0:T(8,128)S(1)}, f32[121,4]{1,0:T(8,128)S(1)}, u32[]{:S(2)}, u32[]{:S(2)}) collective-permute-start(f32[121,4]{1,0:T(8,128)S(1)} %get-tuple-element.5), channel_id=1, source_target_pairs={{0,1},{1,2},{2,3},{4,5},{5,6},{6,7},{8,9},{9,10},{10,11},{12,13},{... | collective-permute-start | bytes 5816 | tf_op jit(solution)/shard_map/ppermute | solution.py:24
  25.7 1.3 %collective-permute-start.1 = (f32[121,4]{1,0:T(8,128)S(1)}, f32[121,4]{1,0:T(8,128)S(1)}, u32[]{:S(2)}, u32[]{:S(2)}) collective-permute-start(f32[121,4]{1,0:T(8,128)S(1)} %get-tuple-element.6), channel_id=1, source_target_pairs={{1,0},{2,1},{3,2},{5,4},{6,5},{7,6},{9,8},{10,9},{11,10},{13,12},{... | collective-permute-start | bytes 5816 | tf_op jit(solution)/shard_map/ppermute | solution.py:25
  27.0 3.6 %collective-permute-done.1 = f32[121,4]{1,0:T(8,128)S(1)} collective-permute-done((f32[121,4]{1,0:T(8,128)S(1)}, f32[121,4]{1,0:T(8,128)S(1)}, u32[]{:S(2)}, u32[]{:S(2)}) %collective-permute-start.1) | collective-permute-done | bytes 1968 | tf_op jit(solution)/shard_map/ppermute | solution.py:25
  30.6 0.1 pad_maximum_fusion.2
  30.8 0.2 fusion.57
  31.0 0.2 fusion.55
  31.3 0.2 fusion.53
  31.7 0.4 fusion.58
  32.1 0.2 copy.28
  32.2 11.7 %all_to_all.35 = f32[2,16,8,256]{3,2,0,1:T(8,128)S(1)} all-to-all(f32[2,16,8,256]{3,2,0,1:T(8,128)S(1)} %copy.28), channel_id=1, replica_groups=mesh['freq'=8,'cell'=4] {'freq'}, dimensions={1} | all-to-all | bytes 524288 | tf_op jit(solution)/shard_map/all_to_all | solution.py:117
  44.0 1.2 %fusion = f32[2,64,600]{2,1,0:T(8,128)S(1)} fusion(f32[2,2,600,256]{3,2,1,0:T(8,128)S(1)} %copy-done, f32[2,2,8,8,256]{4,3,2,1,0:T(8,128)S(1)} %bitcast.100), kind=kOutput, calls=%fused_computation | convolution fusion | flops 235929600 | bytes 1667072 | tf_op jit(solution)/shard_map/kjm,ksm->kjs/dot_general | solution.py:72
  45.2 1.2 %fusion.2 = f32[2,64,600]{2,1,0:T(8,128)S(1)} fusion(f32[2,2,600,256]{3,2,1,0:T(8,128)S(1)} %copy-done, f32[2,2,8,8,256]{4,3,2,1,0:T(8,128)S(1)} %bitcast.101), kind=kOutput, calls=%fused_computation.2 | convolution fusion | flops 235929600 | bytes 1667072 | tf_op jit(solution)/shard_map/kjm,ksm->kjs/dot_general | solution.py:69
  46.4 1.2 %fusion.19 = f32[2,64,600]{2,1,0:T(8,128)S(1)} fusion(f32[2,64,600]{2,1,0:T(8,128)S(1)} %fusion, f32[2,2,600,256]{3,2,1,0:T(8,128)S(1)} %copy-done, f32[2,2,8,8,256]{4,3,2,1,0:T(8,128)S(1)} %bitcast.102), kind=kOutput, calls=%fused_computation.17 | convolution fusion | flops 236006400 | bytes 1994752 | tf_op jit(solution)/shard_map/kjm,ksm->kjs/dot_general | solution.py:72
  47.7 1.2 %fusion.16 = f32[2,64,600]{2,1,0:T(8,128)S(1)} fusion(f32[2,64,600]{2,1,0:T(8,128)S(1)} %fusion.2, f32[2,2,600,256]{3,2,1,0:T(8,128)S(1)} %copy-done, f32[2,2,8,8,256]{4,3,2,1,0:T(8,128)S(1)} %bitcast.103), kind=kOutput, calls=%fused_computation.16 | convolution fusion | flops 236006400 | bytes 1994752 | tf_op jit(solution)/shard_map/kjm,ksm->kjs/dot_general | solution.py:69
  49.0 14.0 %all_to_all.36 = f32[2,2,4,16,600]{4,3,1,0,2:T(8,128)S(1)} all-to-all(f32[2,2,4,16,600]{4,3,1,0,2:T(8,128)S(1)} %copy.33), channel_id=1, replica_groups=mesh['freq'=8,'cell'=4] {'cell'}, dimensions={2} | all-to-all | bytes 1228800 | tf_op jit(solution)/shard_map/all_to_all | solution.py:121
  63.0 0.7 %reduce_sum.19 = f32[2,2,16,600]{3,2,1,0:T(8,128)} reduce(f32[2,2,4,16,600]{4,3,1,0,2:T(8,128)S(1)} %all_to_all.36, f32[]{:T(128)} %constant.26.clone.1), dimensions={2}, to_apply=%region_1.2 | reduce | flops 115200 | bytes 768004 | tf_op jit(solution)/shard_map/reduce_sum | solution.py:122
  (33 shorter events, 1.2 us)
Async XLA Ops:
  0.0 4.8 %copy-start = (f32[2,2,600,256]{3,2,1,0:T(8,128)S(1)}, f32[2,2,600,256]{3,2,1,0:T(8,128)}, u32[]{:S(2)}) copy-start(f32[2,2,600,256]{3,2,1,0:T(8,128)} %param.6) | copy-start | bytes 7372804
  0.0 4.8 %copy-start.1 = (f32[2,2,64,600]{3,2,1,0:T(8,128)S(1)}, f32[2,2,64,600]{3,2,1,0:T(8,128)}, u32[]{:S(2)}) copy-start(f32[2,2,64,600]{3,2,1,0:T(8,128)} %param.5) | copy-start | bytes 1843204
  4.8 10.2 %copy-start.2 = (s32[256]{0:T(256)S(1)}, s32[256]{0:T(256)}, u32[]{:S(2)}) copy-start(s32[256]{0:T(256)} %param.8) | copy-start | bytes 3076
  4.8 10.2 %copy-start.3 = (f32[8]{0:T(128)S(1)}, f32[8]{0:T(128)}, u32[]{:S(2)}) copy-start(f32[8]{0:T(128)} %param.9) | copy-start | bytes 100
  4.8 10.3 %copy-start.4 = (s32[64]{0:T(128)S(1)}, s32[64]{0:T(128)}, u32[]{:S(2)}) copy-start(s32[64]{0:T(128)} %param.7) | copy-start | bytes 772
  7.6 16.2 %all-to-all-start = ((f32[2,2,64,256]{3,1,0,2:T(2,128)}), f32[2,2,64,256]{3,1,0,2:T(2,128)S(1)}, u32[]{:S(2)}, u32[]{:S(2)}) async-start(f32[2,2,64,256]{3,1,0,2:T(2,128)} %copy.23), calls=%async_computation | async-start | bytes 524288 | tf_op jit(solution)/shard_map/all_to_all | solution.py:81
  24.4 2.6 %collective-permute-start = (f32[121,4]{1,0:T(8,128)S(1)}, f32[121,4]{1,0:T(8,128)S(1)}, u32[]{:S(2)}, u32[]{:S(2)}) collective-permute-start(f32[121,4]{1,0:T(8,128)S(1)} %get-tuple-element.5), channel_id=1, source_target_pairs={{0,1},{1,2},{2,3},{4,5},{5,6},{6,7},{8,9},{9,10},{10,11},{12,13},{... | collective-permute-start | bytes 5816 | tf_op jit(solution)/shard_map/ppermute | solution.py:24
  25.7 4.9 %collective-permute-start.1 = (f32[121,4]{1,0:T(8,128)S(1)}, f32[121,4]{1,0:T(8,128)S(1)}, u32[]{:S(2)}, u32[]{:S(2)}) collective-permute-start(f32[121,4]{1,0:T(8,128)S(1)} %get-tuple-element.6), channel_id=1, source_target_pairs={{1,0},{2,1},{3,2},{5,4},{6,5},{7,6},{9,8},{10,9},{11,10},{13,12},{... | collective-permute-start | bytes 5816 | tf_op jit(solution)/shard_map/ppermute | solution.py:25
